TPU v7x, 128 devices: a whole 4x4x4 slice. The times are simulated.
128 devices in a mesh: batch: 32 (over z, y_hi, x), head: 4 (over y_lo, core).
Axes of the slice: x: 4, y: 4 (y_hi: 2, y_lo: 2; y = y_hi * 2 + y_lo), z: 4, core: 2. Of those that a mesh axis runs over, the one named last changes fastest.
Arguments:
- features: bfloat16 [4096, 24, 512], P(('batch', 'head')), may hold values from -6 to 6
- state_h: bfloat16 [4096, 1024], P(('batch', 'head')), may hold values from -0.8984375 to 0.8984375
- state_c: bfloat16 [4096, 1024], P(('batch', 'head')), may hold values from -4 to 4
- valid: int32 [4096], P(('batch', 'head')), may hold values 0 or 1
- ends: int32 [4096, 24], P(('batch', 'head')), may hold values 0 or 1
- policy: int32 [4096, 1], P(('batch', 'head')), may hold values from 0 to 31; in each aligned block of 32 rows (0 to 31, 32 to 63, ...) at most 2 rows name the same one
- actions: int32 [4096, 16], P(('batch', 'head')), may hold values from 0 to 17
- w_input: bfloat16 [512, 4, 1024], P('batch', None, 'head'), may hold values from -0.25 to 0.25
- w_recur: bfloat16 [1024, 4, 1024], P('batch', None, 'head'), may hold values from -0.1875 to 0.1875
- lstm_bias: float32 [4, 1024], replicated, may hold values from -3 to 5
- w_hidden: bfloat16 [32, 1024, 1024], P('head'), may hold values from -0.1875 to 0.1875
- w_value: bfloat16 [32, 512], P('head'), may hold values from -0.25 to 0.25
- w_advantage: bfloat16 [32, 512, 18], P('head'), may hold values from -0.25 to 0.25
Outputs:
- q_values: float32 [4096, 16, 18], P(('batch', 'head'))
- q_taken: float32 [4096, 16], P(('batch', 'head'))
Inputs may be any that keep to these rules, and one draw needn't show every extreme that they name: In the rows of one device no policy appears more than 2 times, and some policy appears exactly 2 times.
All inputs are finite; a program needn't handle non-finite values. No bound on the sum of `valid` or of `ends` on one device may be relied on, other than what follows from the above.
Results may differ from a plain program's by a relative error of at most 0.007.
Values may be sent and summed in bfloat16 or wider, within the bound.
A program may use at most 128 MiB of HBM per device.

v0:
```python
import jax
import jax.numpy as jnp
from jax import lax
from jax.sharding import PartitionSpec as P

ACTIONS = 18
POLICIES = 32
CAPP = 2


def in_one_piece(arrays, axis, dim, along):
    widths = [a.shape[along] for a in arrays]
    both = jnp.concatenate(arrays, axis=along)
    filled = lax.all_gather(both, axis, axis=dim, tiled=True)
    return tuple(jnp.split(filled, [sum(widths[:k]) for k in range(1, len(widths))], axis=along))


def slot_table(owners, per_source, capacity, policies):
    count = owners.shape[0]
    sources = count // per_source
    place = jnp.arange(count, dtype=jnp.int32)
    anchor = place // per_source
    before = (
        (owners[:, None] == owners[None, :])
        & (anchor[:, None] == anchor[None, :])
        & (place[None, :] < place[:, None])
    )
    rank = jnp.sum(before.astype(jnp.int32), axis=1)
    target = owners * (sources * capacity) + anchor * capacity + rank
    total = policies * sources * capacity
    return (jnp.arange(total, dtype=jnp.int32)[:, None] == target[None, :]).astype(jnp.bfloat16)


def lstm_cell(pre_t, full_h, cell_state, keep_t, w_flat, bias, width):
    full_h = full_h * keep_t[:, None].astype(jnp.bfloat16)
    cell_state = cell_state * keep_t[:, None]
    gates = (
        pre_t
        + jnp.dot(full_h, w_flat, preferred_element_type=jnp.float32).reshape(-1, 4, width)
        + bias
    )
    cell_state = jax.nn.sigmoid(gates[:, 1]) * cell_state + jax.nn.sigmoid(gates[:, 0]) * jnp.tanh(
        gates[:, 2]
    )
    new_h = (jax.nn.sigmoid(gates[:, 3]) * jnp.tanh(cell_state)).astype(jnp.bfloat16)
    return (new_h, cell_state)


def shards(
    features,
    state_h,
    state_c,
    valid,
    ends,
    policy,
    actions,
    w_input,
    w_recur,
    lstm_bias,
    w_hidden,
    w_value,
    w_advantage,
):
    seq_dev, steps, width_e = features.shape
    width_h = state_h.shape[1]
    learn = actions.shape[1]
    burn = steps - learn
    keep_start = valid.astype(jnp.bfloat16)[:, None]
    start_h = state_h * keep_start
    start_c = state_c * keep_start
    w_in_rows, w_rec_rows = in_one_piece((w_input, w_recur), "head", 2, 0)
    feat_flat = features.transpose(1, 0, 2).reshape(-1, width_e)
    w_in_full = lax.all_gather(w_in_rows, "batch", axis=0, tiled=True).reshape(width_e, 4 * width_h)
    pre = jnp.dot(feat_flat, w_in_full, preferred_element_type=jnp.float32).reshape(
        steps, seq_dev, 4, width_h
    )
    w_flat = lax.all_gather(w_rec_rows, "batch", axis=0, tiled=True).reshape(width_h, 4 * width_h)
    keeps = 1.0 - ends.astype(jnp.float32).T

    def advance(carry, inputs):
        full_h, cell_state = carry
        pre_t, keep_t = inputs
        new_h, cell_state = lstm_cell(pre_t, full_h, cell_state, keep_t, w_flat, lstm_bias, width_h)
        return ((new_h, cell_state), new_h)

    _, outputs = lax.scan(advance, (start_h, start_c.astype(jnp.float32)), (pre, keeps))
    learned = outputs[burn:]
    table = slot_table(policy[:, 0], seq_dev, CAPP, POLICIES)
    packed = jnp.einsum("ks,tsu->ktu", table, learned, preferred_element_type=jnp.float32).astype(
        jnp.bfloat16
    )
    packed = packed.reshape(POLICIES, CAPP, learn, width_h)
    routed = lax.all_to_all(packed, "head", split_axis=0, concat_axis=1, tiled=True)
    local_heads, slots = (routed.shape[0], routed.shape[1])
    rows = routed.reshape(local_heads, slots * learn, width_h)
    mid = jnp.einsum("prh,phk->prk", rows, w_hidden, preferred_element_type=jnp.float32)
    mid = jnp.maximum(mid, 0.0).astype(jnp.bfloat16)
    branch = w_value.shape[1]
    value = jnp.einsum(
        "prk,pk->pr", mid[:, :, :branch], w_value, preferred_element_type=jnp.float32
    )
    advantage = jnp.einsum(
        "prk,pka->pra", mid[:, :, branch:], w_advantage, preferred_element_type=jnp.float32
    )
    q_local = value[:, :, None] + advantage - jnp.mean(advantage, axis=-1, keepdims=True)
    q_local = q_local.reshape(local_heads, slots, learn, ACTIONS)
    returned = lax.all_to_all(
        q_local.astype(jnp.bfloat16), "head", split_axis=1, concat_axis=0, tiled=True
    ).astype(q_local.dtype)
    own_table = slot_table(policy[:, 0], seq_dev, CAPP, POLICIES).astype(jnp.float32)
    q_values = jnp.dot(
        own_table.T,
        returned.reshape(POLICIES * CAPP, learn * ACTIONS),
        precision=lax.Precision.HIGHEST,
    ).reshape(seq_dev, learn, ACTIONS)
    chosen = actions[:, :, None] == jnp.arange(ACTIONS, dtype=jnp.int32)[None, None, :]
    q_taken = jnp.sum(jnp.where(chosen, q_values, 0.0), axis=-1)
    return (q_values, q_taken)


def solution(mesh):
    return jax.shard_map(
        shards,
        mesh=mesh,
        in_specs=(
            P(("batch", "head"), None, None),
            P(("batch", "head"), None),
            P(("batch", "head"), None),
            P(("batch", "head")),
            P(("batch", "head"), None),
            P(("batch", "head"), None),
            P(("batch", "head"), None),
            P("batch", None, "head"),
            P("batch", None, "head"),
            P(),
            P("head", None, None),
            P("head", None),
            P("head", None, None),
        ),
        out_specs=(P(("batch", "head"), None, None), P(("batch", "head"), None)),
        check_vma=False,
    )
```

profile of v0, /device:TPU:1, one launch (start us, length us, event | category | flops | bytes accessed | tf_op | source)
XLA Modules:
  0.0 450.7 jit_solution(334485971511818191)
XLA Ops:
  7.3 1.0 pad_maximum_fusion
  8.3 7.9 %all_gather.9 = bf16[48,4,1024]{2,1,0:T(4,128)(2,1)S(1)} all-gather(bf16[48,4,256]{2,1,0:T(4,128)(2,1)S(1)} %pad_maximum_fusion), channel_id=1, replica_groups=mesh['batch'=32,'head'=4] {'head'}, dimensions={2}, use_global_device_ids=true | all-gather | bytes 491520 | tf_op jit(solution)/shard_map/all_gather | solution.py:14
  18.4 79.2 %all-gather.3.cloned.1.call-done = bf16[512,4,1024]{2,1,0:T(4,128)(2,1)} async-done(((bf16[16,4,1024]{2,1,0:T(4,128)(2,1)}), bf16[512,4,1024]{2,1,0:T(4,128)(2,1)}) %all-gather.3.cloned.1.call-update) | async-done | bytes 4194320 | tf_op jit(solution)/shard_map/all_gather | solution.py:73
  97.6 4.5 copy.61
  102.1 6.6 %convolution_bitcast_fusion = f32[768,4096]{0,1:T(8,128)} fusion(bf16[512,4096]{1,0:T(8,128)(2,1)S(1)} %bitcast.92, bf16[768,512]{1,0:T(8,128)(2,1)S(1)} %bitcast.96), kind=kOutput, calls=%fused_computation.30 | convolution fusion | flops 3221225472 | bytes 17563648 | tf_op jit(solution)/shard_map/dot_general | solution.py:74
  108.7 12.7 %copy.47 = f32[768,4096]{1,0:T(8,128)} copy(f32[768,4096]{0,1:T(8,128)} %convolution_bitcast_fusion) | data formatting | bytes 25165824 | tf_op jit(solution)/shard_map/dot_general | solution.py:74
  121.3 15.6 %reshape.110 = f32[24,32,4,1024]{3,2,1,0:T(4,128)} reshape(f32[768,4096]{1,0:T(8,128)} %copy.47) | data formatting | bytes 25165824 | tf_op jit(solution)/shard_map/reshape | solution.py:74
  137.0 65.1 %all-gather.5.cloned.1.call-done = bf16[1024,4,1024]{2,1,0:T(4,128)(2,1)} async-done(((bf16[32,4,1024]{2,1,0:T(4,128)(2,1)}), bf16[1024,4,1024]{2,1,0:T(4,128)(2,1)}) %all-gather.5.cloned.1.call-update) | async-done | bytes 8388624 | tf_op jit(solution)/shard_map/all_gather | solution.py:77
  202.1 12.1 %copy.62 = bf16[128,8,4,1024]{3,1,2,0:T(8,128)(2,1)} copy(bf16[128,8,4,1024]{3,2,1,0:T(4,128)(2,1)} %bitcast.89) | data formatting | bytes 16777216
  214.2 173.0 %while.14 = (s32[]{:T(128)}, bf16[32,1024]{1,0:T(8,128)(2,1)S(1)}, f32[32,1024]{1,0:T(8,128)S(1)}, bf16[24,32,1024]{2,1,0:T(8,128)(2,1)}, f32[24,32,4,1024]{3,2,...) while((s32[]{:T(128)}, bf16[32,1024]{1,0:T(8,128)(2,1)S(1)}, ...), condition=%wide.region_2.3_spmd, body=%wide.region_1.2_spmd.sunk | while | flops 269221920 | bytes 12534885 | solution.py:86
  214.2 5.0 %fusion.55 = f32[32,4096]{1,0:T(8,128)S(1)} fusion(bf16[1024,4096]{1,0:T(8,128)(2,1)} %get-tuple-element.171, bf16[32,1024]{1,0:T(8,128)(2,1)S(1)} %get-tuple-element.157, bf16[32]{0:T(256)(128)(2,1)S(1)} %get-tuple-element.142), kind=kOutput, calls=%fused_computation.24.clone.1 | convolution fusion | flops 268468224 | bytes 8978496 | tf_op jit(solution)/shard_map/while/body/eval_jaxpr/dot_general | solution.py:39
  219.2 1.1 constant_dynamic-slice_fusion.3
  221.4 5.0 %fusion.55 = f32[32,4096]{1,0:T(8,128)S(1)} fusion(bf16[1024,4096]{1,0:T(8,128)(2,1)} %get-tuple-element.171, bf16[32,1024]{1,0:T(8,128)(2,1)S(1)} %get-tuple-element.157, bf16[32]{0:T(256)(128)(2,1)S(1)} %get-tuple-element.142), kind=kOutput, calls=%fused_computation.24.clone.1 | convolution fusion | flops 268468224 | bytes 8978496 | tf_op jit(solution)/shard_map/while/body/eval_jaxpr/dot_general | solution.py:39
  226.4 1.1 constant_dynamic-slice_fusion.3
  228.6 5.0 %fusion.55 = f32[32,4096]{1,0:T(8,128)S(1)} fusion(bf16[1024,4096]{1,0:T(8,128)(2,1)} %get-tuple-element.171, bf16[32,1024]{1,0:T(8,128)(2,1)S(1)} %get-tuple-element.157, bf16[32]{0:T(256)(128)(2,1)S(1)} %get-tuple-element.142), kind=kOutput, calls=%fused_computation.24.clone.1 | convolution fusion | flops 268468224 | bytes 8978496 | tf_op jit(solution)/shard_map/while/body/eval_jaxpr/dot_general | solution.py:39
  233.6 1.1 constant_dynamic-slice_fusion.3
  235.8 5.0 %fusion.55 = f32[32,4096]{1,0:T(8,128)S(1)} fusion(bf16[1024,4096]{1,0:T(8,128)(2,1)} %get-tuple-element.171, bf16[32,1024]{1,0:T(8,128)(2,1)S(1)} %get-tuple-element.157, bf16[32]{0:T(256)(128)(2,1)S(1)} %get-tuple-element.142), kind=kOutput, calls=%fused_computation.24.clone.1 | convolution fusion | flops 268468224 | bytes 8978496 | tf_op jit(solution)/shard_map/while/body/eval_jaxpr/dot_general | solution.py:39
  240.8 1.1 constant_dynamic-slice_fusion.3
  243.0 5.0 %fusion.55 = f32[32,4096]{1,0:T(8,128)S(1)} fusion(bf16[1024,4096]{1,0:T(8,128)(2,1)} %get-tuple-element.171, bf16[32,1024]{1,0:T(8,128)(2,1)S(1)} %get-tuple-element.157, bf16[32]{0:T(256)(128)(2,1)S(1)} %get-tuple-element.142), kind=kOutput, calls=%fused_computation.24.clone.1 | convolution fusion | flops 268468224 | bytes 8978496 | tf_op jit(solution)/shard_map/while/body/eval_jaxpr/dot_general | solution.py:39
  248.0 1.1 constant_dynamic-slice_fusion.3
  250.2 5.0 %fusion.55 = f32[32,4096]{1,0:T(8,128)S(1)} fusion(bf16[1024,4096]{1,0:T(8,128)(2,1)} %get-tuple-element.171, bf16[32,1024]{1,0:T(8,128)(2,1)S(1)} %get-tuple-element.157, bf16[32]{0:T(256)(128)(2,1)S(1)} %get-tuple-element.142), kind=kOutput, calls=%fused_computation.24.clone.1 | convolution fusion | flops 268468224 | bytes 8978496 | tf_op jit(solution)/shard_map/while/body/eval_jaxpr/dot_general | solution.py:39
  255.2 1.1 constant_dynamic-slice_fusion.3
  257.4 5.0 %fusion.55 = f32[32,4096]{1,0:T(8,128)S(1)} fusion(bf16[1024,4096]{1,0:T(8,128)(2,1)} %get-tuple-element.171, bf16[32,1024]{1,0:T(8,128)(2,1)S(1)} %get-tuple-element.157, bf16[32]{0:T(256)(128)(2,1)S(1)} %get-tuple-element.142), kind=kOutput, calls=%fused_computation.24.clone.1 | convolution fusion | flops 268468224 | bytes 8978496 | tf_op jit(solution)/shard_map/while/body/eval_jaxpr/dot_general | solution.py:39
  262.4 1.1 constant_dynamic-slice_fusion.3
  264.6 5.0 %fusion.55 = f32[32,4096]{1,0:T(8,128)S(1)} fusion(bf16[1024,4096]{1,0:T(8,128)(2,1)} %get-tuple-element.171, bf16[32,1024]{1,0:T(8,128)(2,1)S(1)} %get-tuple-element.157, bf16[32]{0:T(256)(128)(2,1)S(1)} %get-tuple-element.142), kind=kOutput, calls=%fused_computation.24.clone.1 | convolution fusion | flops 268468224 | bytes 8978496 | tf_op jit(solution)/shard_map/while/body/eval_jaxpr/dot_general | solution.py:39
  269.6 1.1 constant_dynamic-slice_fusion.3
  271.9 5.0 %fusion.55 = f32[32,4096]{1,0:T(8,128)S(1)} fusion(bf16[1024,4096]{1,0:T(8,128)(2,1)} %get-tuple-element.171, bf16[32,1024]{1,0:T(8,128)(2,1)S(1)} %get-tuple-element.157, bf16[32]{0:T(256)(128)(2,1)S(1)} %get-tuple-element.142), kind=kOutput, calls=%fused_computation.24.clone.1 | convolution fusion | flops 268468224 | bytes 8978496 | tf_op jit(solution)/shard_map/while/body/eval_jaxpr/dot_general | solution.py:39
  276.8 1.1 constant_dynamic-slice_fusion.3
  279.1 5.0 %fusion.55 = f32[32,4096]{1,0:T(8,128)S(1)} fusion(bf16[1024,4096]{1,0:T(8,128)(2,1)} %get-tuple-element.171, bf16[32,1024]{1,0:T(8,128)(2,1)S(1)} %get-tuple-element.157, bf16[32]{0:T(256)(128)(2,1)S(1)} %get-tuple-element.142), kind=kOutput, calls=%fused_computation.24.clone.1 | convolution fusion | flops 268468224 | bytes 8978496 | tf_op jit(solution)/shard_map/while/body/eval_jaxpr/dot_general | solution.py:39
  284.0 1.1 constant_dynamic-slice_fusion.3
  286.3 5.0 %fusion.55 = f32[32,4096]{1,0:T(8,128)S(1)} fusion(bf16[1024,4096]{1,0:T(8,128)(2,1)} %get-tuple-element.171, bf16[32,1024]{1,0:T(8,128)(2,1)S(1)} %get-tuple-element.157, bf16[32]{0:T(256)(128)(2,1)S(1)} %get-tuple-element.142), kind=kOutput, calls=%fused_computation.24.clone.1 | convolution fusion | flops 268468224 | bytes 8978496 | tf_op jit(solution)/shard_map/while/body/eval_jaxpr/dot_general | solution.py:39
  291.2 1.1 constant_dynamic-slice_fusion.3
  293.5 5.0 %fusion.55 = f32[32,4096]{1,0:T(8,128)S(1)} fusion(bf16[1024,4096]{1,0:T(8,128)(2,1)} %get-tuple-element.171, bf16[32,1024]{1,0:T(8,128)(2,1)S(1)} %get-tuple-element.157, bf16[32]{0:T(256)(128)(2,1)S(1)} %get-tuple-element.142), kind=kOutput, calls=%fused_computation.24.clone.1 | convolution fusion | flops 268468224 | bytes 8978496 | tf_op jit(solution)/shard_map/while/body/eval_jaxpr/dot_general | solution.py:39
  298.5 1.1 constant_dynamic-slice_fusion.3
  300.7 5.0 %fusion.55 = f32[32,4096]{1,0:T(8,128)S(1)} fusion(bf16[1024,4096]{1,0:T(8,128)(2,1)} %get-tuple-element.171, bf16[32,1024]{1,0:T(8,128)(2,1)S(1)} %get-tuple-element.157, bf16[32]{0:T(256)(128)(2,1)S(1)} %get-tuple-element.142), kind=kOutput, calls=%fused_computation.24.clone.1 | convolution fusion | flops 268468224 | bytes 8978496 | tf_op jit(solution)/shard_map/while/body/eval_jaxpr/dot_general | solution.py:39
  305.7 1.1 constant_dynamic-slice_fusion.3
  307.9 5.0 %fusion.55 = f32[32,4096]{1,0:T(8,128)S(1)} fusion(bf16[1024,4096]{1,0:T(8,128)(2,1)} %get-tuple-element.171, bf16[32,1024]{1,0:T(8,128)(2,1)S(1)} %get-tuple-element.157, bf16[32]{0:T(256)(128)(2,1)S(1)} %get-tuple-element.142), kind=kOutput, calls=%fused_computation.24.clone.1 | convolution fusion | flops 268468224 | bytes 8978496 | tf_op jit(solution)/shard_map/while/body/eval_jaxpr/dot_general | solution.py:39
  312.9 1.1 constant_dynamic-slice_fusion.3
  315.1 5.0 %fusion.55 = f32[32,4096]{1,0:T(8,128)S(1)} fusion(bf16[1024,4096]{1,0:T(8,128)(2,1)} %get-tuple-element.171, bf16[32,1024]{1,0:T(8,128)(2,1)S(1)} %get-tuple-element.157, bf16[32]{0:T(256)(128)(2,1)S(1)} %get-tuple-element.142), kind=kOutput, calls=%fused_computation.24.clone.1 | convolution fusion | flops 268468224 | bytes 8978496 | tf_op jit(solution)/shard_map/while/body/eval_jaxpr/dot_general | solution.py:39
  320.1 1.1 constant_dynamic-slice_fusion.3
  322.3 5.0 %fusion.55 = f32[32,4096]{1,0:T(8,128)S(1)} fusion(bf16[1024,4096]{1,0:T(8,128)(2,1)} %get-tuple-element.171, bf16[32,1024]{1,0:T(8,128)(2,1)S(1)} %get-tuple-element.157, bf16[32]{0:T(256)(128)(2,1)S(1)} %get-tuple-element.142), kind=kOutput, calls=%fused_computation.24.clone.1 | convolution fusion | flops 268468224 | bytes 8978496 | tf_op jit(solution)/shard_map/while/body/eval_jaxpr/dot_general | solution.py:39
  327.3 1.1 constant_dynamic-slice_fusion.3
  329.5 5.0 %fusion.55 = f32[32,4096]{1,0:T(8,128)S(1)} fusion(bf16[1024,4096]{1,0:T(8,128)(2,1)} %get-tuple-element.171, bf16[32,1024]{1,0:T(8,128)(2,1)S(1)} %get-tuple-element.157, bf16[32]{0:T(256)(128)(2,1)S(1)} %get-tuple-element.142), kind=kOutput, calls=%fused_computation.24.clone.1 | convolution fusion | flops 268468224 | bytes 8978496 | tf_op jit(solution)/shard_map/while/body/eval_jaxpr/dot_general | solution.py:39
  334.5 1.1 constant_dynamic-slice_fusion.3
  336.7 5.0 %fusion.55 = f32[32,4096]{1,0:T(8,128)S(1)} fusion(bf16[1024,4096]{1,0:T(8,128)(2,1)} %get-tuple-element.171, bf16[32,1024]{1,0:T(8,128)(2,1)S(1)} %get-tuple-element.157, bf16[32]{0:T(256)(128)(2,1)S(1)} %get-tuple-element.142), kind=kOutput, calls=%fused_computation.24.clone.1 | convolution fusion | flops 268468224 | bytes 8978496 | tf_op jit(solution)/shard_map/while/body/eval_jaxpr/dot_general | solution.py:39
  341.7 1.1 constant_dynamic-slice_fusion.3
  344.0 5.0 %fusion.55 = f32[32,4096]{1,0:T(8,128)S(1)} fusion(bf16[1024,4096]{1,0:T(8,128)(2,1)} %get-tuple-element.171, bf16[32,1024]{1,0:T(8,128)(2,1)S(1)} %get-tuple-element.157, bf16[32]{0:T(256)(128)(2,1)S(1)} %get-tuple-element.142), kind=kOutput, calls=%fused_computation.24.clone.1 | convolution fusion | flops 268468224 | bytes 8978496 | tf_op jit(solution)/shard_map/while/body/eval_jaxpr/dot_general | solution.py:39
  348.9 1.1 constant_dynamic-slice_fusion.3
  351.2 5.0 %fusion.55 = f32[32,4096]{1,0:T(8,128)S(1)} fusion(bf16[1024,4096]{1,0:T(8,128)(2,1)} %get-tuple-element.171, bf16[32,1024]{1,0:T(8,128)(2,1)S(1)} %get-tuple-element.157, bf16[32]{0:T(256)(128)(2,1)S(1)} %get-tuple-element.142), kind=kOutput, calls=%fused_computation.24.clone.1 | convolution fusion | flops 268468224 | bytes 8978496 | tf_op jit(solution)/shard_map/while/body/eval_jaxpr/dot_general | solution.py:39
  356.1 1.1 constant_dynamic-slice_fusion.3
  358.4 5.0 %fusion.55 = f32[32,4096]{1,0:T(8,128)S(1)} fusion(bf16[1024,4096]{1,0:T(8,128)(2,1)} %get-tuple-element.171, bf16[32,1024]{1,0:T(8,128)(2,1)S(1)} %get-tuple-element.157, bf16[32]{0:T(256)(128)(2,1)S(1)} %get-tuple-element.142), kind=kOutput, calls=%fused_computation.24.clone.1 | convolution fusion | flops 268468224 | bytes 8978496 | tf_op jit(solution)/shard_map/while/body/eval_jaxpr/dot_general | solution.py:39
  363.3 1.1 constant_dynamic-slice_fusion.3
  365.6 5.0 %fusion.55 = f32[32,4096]{1,0:T(8,128)S(1)} fusion(bf16[1024,4096]{1,0:T(8,128)(2,1)} %get-tuple-element.171, bf16[32,1024]{1,0:T(8,128)(2,1)S(1)} %get-tuple-element.157, bf16[32]{0:T(256)(128)(2,1)S(1)} %get-tuple-element.142), kind=kOutput, calls=%fused_computation.24.clone.1 | convolution fusion | flops 268468224 | bytes 8978496 | tf_op jit(solution)/shard_map/while/body/eval_jaxpr/dot_general | solution.py:39
  370.5 1.1 constant_dynamic-slice_fusion.3
  372.8 5.0 %fusion.55 = f32[32,4096]{1,0:T(8,128)S(1)} fusion(bf16[1024,4096]{1,0:T(8,128)(2,1)} %get-tuple-element.171, bf16[32,1024]{1,0:T(8,128)(2,1)S(1)} %get-tuple-element.157, bf16[32]{0:T(256)(128)(2,1)S(1)} %get-tuple-element.142), kind=kOutput, calls=%fused_computation.24.clone.1 | convolution fusion | flops 268468224 | bytes 8978496 | tf_op jit(solution)/shard_map/while/body/eval_jaxpr/dot_general | solution.py:39
  377.8 1.1 constant_dynamic-slice_fusion.3
  380.0 5.0 %fusion.55 = f32[32,4096]{1,0:T(8,128)S(1)} fusion(bf16[1024,4096]{1,0:T(8,128)(2,1)} %get-tuple-element.171, bf16[32,1024]{1,0:T(8,128)(2,1)S(1)} %get-tuple-element.157, bf16[32]{0:T(256)(128)(2,1)S(1)} %get-tuple-element.142), kind=kOutput, calls=%fused_computation.24.clone.1 | convolution fusion | flops 268468224 | bytes 8978496 | tf_op jit(solution)/shard_map/while/body/eval_jaxpr/dot_general | solution.py:39
  385.0 1.1 constant_dynamic-slice_fusion.3
  387.2 2.0 convolution_convert_fusion
  389.2 2.2 reshape.112
  391.5 3.8 copy.48
  395.2 28.5 %all_to_all.30 = bf16[32,2,16,1024]{3,1,2,0:T(2,128)(2,1)S(1)} all-to-all(bf16[32,2,16,1024]{3,1,2,0:T(2,128)(2,1)S(1)} %copy.48), channel_id=1, replica_groups=mesh['batch'=32,'head'=4] {'head'}, dimensions={0} | all-to-all | bytes 4194304 | tf_op jit(solution)/shard_map/all_to_all | solution.py:93
  424.4 8.3 %maximum_convert_fusion = bf16[8,128,1024]{2,1,0:T(8,128)(2,1)S(1)} fusion(bf16[8,128,1024]{2,1,0:T(8,128)(2,1)S(1)} %bitcast.88, bf16[8,1024,1024]{2,1,0:T(8,128)(2,1)} %param.25), kind=kOutput, calls=%fused_computation.31 | convolution fusion | flops 2149580800 | bytes 20971520 | tf_op jit(solution)/shard_map/prh,phk->prk/dot_general | solution.py:96
  434.7 6.6 %all_to_all.31 = bf16[4,2,2304]{2,1,0:T(2,128)(2,1)S(1)} all-to-all(bf16[4,2,2304]{2,1,0:T(2,128)(2,1)S(1)} %reshape.120), channel_id=1, replica_groups=mesh['batch'=32,'head'=4] {'head'}, dimensions={0} | all-to-all | bytes 73728 | tf_op jit(solution)/shard_map/all_to_all | solution.py:107
  (121 shorter events, 34.8 us)
Async XLA Ops:
  7.2 425.5 %copy-start = (bf16[8,512,18]{1,0,2:T(8,128)(2,1)S(1)}, bf16[8,512,18]{1,0,2:T(8,128)(2,1)}, u32[]{:S(2)}) copy-start(bf16[8,512,18]{1,0,2:T(8,128)(2,1)} %param.27) | copy-start | bytes 442372
  7.2 10.6 %copy-start.1 = (bf16[32,24,512]{2,1,0:T(8,128)(2,1)S(1)}, bf16[32,24,512]{2,1,0:T(8,128)(2,1)}, u32[]{:S(2)}) copy-start(bf16[32,24,512]{2,1,0:T(8,128)(2,1)} %param.15) | copy-start | bytes 2359300
  7.2 10.9 %copy-start.9 = (s32[32]{0:T(128)S(1)}, s32[32]{0:T(128)}, u32[]{:S(2)}) copy-start(s32[32]{0:T(128)} %param.18) | copy-start | bytes 388
  7.2 10.9 %copy-start.7 = (s32[32,1]{0,1:T(1,128)S(1)}, s32[32,1]{0,1:T(1,128)}, u32[]{:S(2)}) copy-start(s32[32,1]{0,1:T(1,128)} %param.20) | copy-start | bytes 388
  7.2 11.1 %copy-start.5 = (s32[32,24]{0,1:T(8,128)S(1)}, s32[32,24]{0,1:T(8,128)}, u32[]{:S(2)}) copy-start(s32[32,24]{0,1:T(8,128)} %param.19) | copy-start | bytes 9220
  7.2 11.1 %copy-start.4 = (bf16[32,1024]{1,0:T(8,128)(2,1)S(1)}, bf16[32,1024]{1,0:T(8,128)(2,1)}, u32[]{:S(2)}) copy-start(bf16[32,1024]{1,0:T(8,128)(2,1)} %param.16) | copy-start | bytes 196612
  7.2 11.1 %copy-start.3 = (bf16[32,1024]{1,0:T(8,128)(2,1)S(1)}, bf16[32,1024]{1,0:T(8,128)(2,1)}, u32[]{:S(2)}) copy-start(bf16[32,1024]{1,0:T(8,128)(2,1)} %param.17) | copy-start | bytes 196612
  7.2 90.3 %all-gather.3.cloned.1.call-start = ((), (), s32[]{:S(2)}) async-start(), calls=%async_computation.2 | async-start | bytes 4325376 | tf_op jit(solution)/shard_map/all_gather | solution.py:73
  16.9 185.2 %all-gather.5.cloned.1.call-start = ((), (), s32[]{:S(2)}) async-start(), calls=%async_computation.3 | async-start | bytes 8650752 | tf_op jit(solution)/shard_map/all_gather | solution.py:77
  202.1 12.1 %copy-start.2 = (f32[4,1024]{1,0:T(4,128)S(1)}, f32[4,1024]{1,0:T(4,128)}, u32[]{:S(2)}) copy-start(f32[4,1024]{1,0:T(4,128)} %param.24) | copy-start | bytes 49156
  424.4 8.7 %copy-start.8 = (bf16[8,512]{1,0:T(8,128)(2,1)S(1)}, bf16[8,512]{1,0:T(8,128)(2,1)}, u32[]{:S(2)}) copy-start(bf16[8,512]{1,0:T(8,128)(2,1)} %param.26) | copy-start | bytes 24580
  433.1 9.2 %copy-start.6 = (s32[32,16]{0,1:T(8,128)S(1)}, s32[32,16]{0,1:T(8,128)}, u32[]{:S(2)}) copy-start(s32[32,16]{0,1:T(8,128)} %param.21) | copy-start | bytes 6148
Sparse Core Ops, SparseCore 0:
  17.0 80.4 all-gather.2
  100.6 101.4 all-gather.4
where the time goes:
time: 454 us; the launch traced here: 451 us
  waiting for transfers between devices  144 us (32%)
  matrix products  138 us (30%)
  local copies, waits for them, and re-layouts  82.2 us (18%)
  blocking collectives  43 us (9%)
  other arithmetic  28.7 us (6%)
  between operations  14.3 us (3%)
    dot_general x24, matrix products, lstm_cell(): jnp.dot(full_h, w_flat, preferred_element_type=jnp.float32)  119 us
    all_gather x1, waiting for transfers between devices, shards(): lax.all_gather(w_in_rows, 'batch', axis=0, tiled=True)  79.2 us
    all_gather x1, waiting for transfers between devices, shards(): lax.all_gather(w_rec_rows, 'batch', axis=0, tiled=True)  65.1 us
    all_to_all x1, blocking collectives, shards(): lax.all_to_all(packed, 'head', split_axis=0, concat_axis=1, tiled=True)  28.5 us
    dynamic_slice x24, local copies, waits for them, and re-layouts, shards(): lax.scan(advance, (start_h, start_c.astype(jnp.float32)), (pre, keeps))  26 us
    dynamic_update_slice x24, other arithmetic, shards(): lax.scan(advance, (start_h, start_c.astype(jnp.float32)), (pre, keeps))  19 us
    unnamed x26, local copies, waits for them, and re-layouts  18.5 us
    reshape x1, local copies, waits for them, and re-layouts, shards(): jnp.dot(feat_flat, w_in_full, preferred_element_type=jnp.float32)  15.6 us
  transfers between devices with their start and end apart: 2, of which 2 were waited for; matrix products, arithmetic and copies ran while one was open for 9% of the time, Pallas kernels for 0%

commit v1 on v0

--- a/solution.py
+++ b/solution.py
@@ -6,6 +6,13 @@
 ACTIONS = 18
 POLICIES = 32
 CAPP = 2
+
+
+def bring_the_panels(piece_in, which_dim):
+    samples = []
+    for _ in range(lax.axis_size("batch")):
+        samples.append(piece_in)
+    return jnp.concatenate(lax.all_to_all(jnp.stack(samples, axis=0), "batch", 0, 0), which_dim)
 
 
 def in_one_piece(arrays, axis, dim, along):
@@ -74,7 +81,7 @@
     pre = jnp.dot(feat_flat, w_in_full, preferred_element_type=jnp.float32).reshape(
         steps, seq_dev, 4, width_h
     )
-    w_flat = lax.all_gather(w_rec_rows, "batch", axis=0, tiled=True).reshape(width_h, 4 * width_h)
+    w_flat = bring_the_panels(w_rec_rows, 0).reshape(width_h, 4 * width_h)
     keeps = 1.0 - ends.astype(jnp.float32).T
 
     def advance(carry, inputs):

time: 454 us -> 480 us (1.057)
  starting transfers between devices: 0.08 us -> 10.7 us
  waiting for transfers between devices: 144 us -> 153 us
  local copies, waits for them, and re-layouts: 82.2 us -> 88.6 us
    all_gather x1, waiting for transfers between devices: 79.2 us -> 153 us  [shards(): lax.all_gather(w_in_rows, 'batch', axis=0, tiled=True)]
    all_gather x1 -> x0, waiting for transfers between devices: 65.1 us -> none  [shards(): lax.all_gather(w_rec_rows, 'batch', axis=0, tiled=True)]
    all_to_all x0 -> x1, starting transfers between devices: none -> 10.7 us  [bring_the_panels(): lax.all_to_all(jnp.stack(samples, axis=0), 'batch', 0, 0)]
    another operation x0 -> x1, local copies, waits for them, and re-layouts: none -> 7.12 us  [bring_the_panels(): jnp.stack(samples, axis=0)]
  transfers between devices with their start and end apart: 2 -> 2, of which waited for: 2 -> 1; matrix products, arithmetic and copies ran while one was open for 9% -> 10% of each run, Pallas kernels for 0% -> 0%
where the time goes in v1:
time: 480 us; the launch traced here: 477 us
  waiting for transfers between devices  153 us (32%)
  matrix products  138 us (29%)
  local copies, waits for them, and re-layouts  88.6 us (18%)
  blocking collectives  43 us (9%)
  other arithmetic  28.8 us (6%)
  between operations  14.3 us (3%)
  starting transfers between devices  10.7 us (2%)
    all_gather x1, waiting for transfers between devices, shards(): lax.all_gather(w_in_rows, 'batch', axis=0, tiled=True)  153 us
    dot_general x24, matrix products, lstm_cell(): jnp.dot(full_h, w_flat, preferred_element_type=jnp.float32)  119 us
    all_to_all x1, blocking collectives, shards(): lax.all_to_all(packed, 'head', split_axis=0, concat_axis=1, tiled=True)  28.5 us
    dynamic_slice x24, local copies, waits for them, and re-layouts, shards(): lax.scan(advance, (start_h, start_c.astype(jnp.float32)), (pre, keeps))  26 us
    dynamic_update_slice x24, other arithmetic, shards(): lax.scan(advance, (start_h, start_c.astype(jnp.float32)), (pre, keeps))  19.1 us
    unnamed x26, local copies, waits for them, and re-layouts  18.5 us
    reshape x1, local copies, waits for them, and re-layouts, shards(): jnp.dot(feat_flat, w_in_full, preferred_element_type=jnp.float32)  15.6 us
    dot_general x1, local copies, waits for them, and re-layouts, shards(): jnp.dot(feat_flat, w_in_full, preferred_element_type=jnp.float32)  12.7 us
  transfers between devices with their start and end apart: 2, of which 1 were waited for; matrix products, arithmetic and copies ran while one was open for 10% of the time, Pallas kernels for 0%

profile of v1, /device:TPU:1, one launch (start us, length us, event | category | flops | bytes accessed | tf_op | source)
XLA Modules:
  0.0 476.6 jit_solution(2480667240800114405)
XLA Ops:
  8.2 7.9 %all_gather.6 = bf16[48,4,1024]{2,1,0:T(4,128)(2,1)S(1)} all-gather(bf16[48,4,256]{2,1,0:T(4,128)(2,1)S(1)} %pad_maximum_fusion), channel_id=1, replica_groups=mesh['batch'=32,'head'=4] {'head'}, dimensions={2}, use_global_device_ids=true | all-gather | bytes 491520 | tf_op jit(solution)/shard_map/all_gather | solution.py:21
  16.9 7.1 %stack.2 = bf16[32,32,4,1024]{3,2,1,0:T(4,128)(2,1)} broadcast(bf16[32,4,1024]{2,1,0:T(4,128)(2,1)S(1)} %split.9), dimensions={1,2,3} | broadcast | bytes 8650752 | tf_op jit(solution)/shard_map/stack | solution.py:15
  24.1 10.7 %all-to-all-start = ((bf16[32,32,4,1024]{3,2,1,0:T(4,128)(2,1)}), bf16[32,32,4,1024]{3,2,1,0:T(4,128)(2,1)}, u32[]{:S(2)}, u32[]{:S(2)}) async-start(bf16[32,32,4,1024]{3,2,1,0:T(4,128)(2,1)} %stack.2), calls=%async_computation | async-start | bytes 16777216 | tf_op jit(solution)/shard_map/all_to_all | solution.py:15
  35.4 153.2 %all-gather.2.cloned.1.call-done = bf16[512,4,1024]{2,1,0:T(4,128)(2,1)} async-done(((bf16[16,4,1024]{2,1,0:T(4,128)(2,1)}), bf16[512,4,1024]{2,1,0:T(4,128)(2,1)}) %all-gather.2.cloned.1.call-update) | async-done | bytes 4194320 | tf_op jit(solution)/shard_map/all_gather | solution.py:80
  188.6 4.5 copy.61
  193.1 6.4 %convolution_bitcast_fusion = f32[768,4096]{0,1:T(8,128)} fusion(bf16[512,4096]{1,0:T(8,128)(2,1)S(1)} %bitcast.92, bf16[768,512]{1,0:T(8,128)(2,1)S(1)} %bitcast.96), kind=kOutput, calls=%fused_computation.30 | convolution fusion | flops 3221225472 | bytes 17563648 | tf_op jit(solution)/shard_map/dot_general | solution.py:81
  199.5 12.7 %copy.47 = f32[768,4096]{1,0:T(8,128)} copy(f32[768,4096]{0,1:T(8,128)} %convolution_bitcast_fusion) | data formatting | bytes 25165824 | tf_op jit(solution)/shard_map/dot_general | solution.py:81
  212.2 15.6 %reshape.109 = f32[24,32,4,1024]{3,2,1,0:T(4,128)} reshape(f32[768,4096]{1,0:T(8,128)} %copy.47) | data formatting | bytes 25165824 | tf_op jit(solution)/shard_map/reshape | solution.py:81
  227.8 12.1 %copy.62 = bf16[128,8,4,1024]{3,1,2,0:T(8,128)(2,1)} copy(bf16[128,8,4,1024]{3,2,1,0:T(4,128)(2,1)} %bitcast.28) | data formatting | bytes 16777216
  239.9 173.2 %while.14 = (s32[]{:T(128)}, bf16[32,1024]{1,0:T(8,128)(2,1)S(1)}, f32[32,1024]{1,0:T(8,128)S(1)}, bf16[24,32,1024]{2,1,0:T(8,128)(2,1)}, f32[24,32,4,1024]{3,2,...) while((s32[]{:T(128)}, bf16[32,1024]{1,0:T(8,128)(2,1)S(1)}, ...), condition=%wide.region_2.3_spmd, body=%wide.region_1.2_spmd.sunk | while | flops 269221920 | bytes 12534885 | solution.py:93
  239.9 5.0 %fusion.55 = f32[32,4096]{1,0:T(8,128)S(1)} fusion(bf16[1024,4096]{1,0:T(8,128)(2,1)} %get-tuple-element.171, bf16[32,1024]{1,0:T(8,128)(2,1)S(1)} %get-tuple-element.157, bf16[32]{0:T(256)(128)(2,1)S(1)} %get-tuple-element.142), kind=kOutput, calls=%fused_computation.24.clone.1 | convolution fusion | flops 268468224 | bytes 8978496 | tf_op jit(solution)/shard_map/while/body/eval_jaxpr/dot_general | solution.py:46
  244.9 1.1 constant_dynamic-slice_fusion.3
  247.1 5.0 %fusion.55 = f32[32,4096]{1,0:T(8,128)S(1)} fusion(bf16[1024,4096]{1,0:T(8,128)(2,1)} %get-tuple-element.171, bf16[32,1024]{1,0:T(8,128)(2,1)S(1)} %get-tuple-element.157, bf16[32]{0:T(256)(128)(2,1)S(1)} %get-tuple-element.142), kind=kOutput, calls=%fused_computation.24.clone.1 | convolution fusion | flops 268468224 | bytes 8978496 | tf_op jit(solution)/shard_map/while/body/eval_jaxpr/dot_general | solution.py:46
  252.1 1.1 constant_dynamic-slice_fusion.3
  254.4 5.0 %fusion.55 = f32[32,4096]{1,0:T(8,128)S(1)} fusion(bf16[1024,4096]{1,0:T(8,128)(2,1)} %get-tuple-element.171, bf16[32,1024]{1,0:T(8,128)(2,1)S(1)} %get-tuple-element.157, bf16[32]{0:T(256)(128)(2,1)S(1)} %get-tuple-element.142), kind=kOutput, calls=%fused_computation.24.clone.1 | convolution fusion | flops 268468224 | bytes 8978496 | tf_op jit(solution)/shard_map/while/body/eval_jaxpr/dot_general | solution.py:46
  259.3 1.1 constant_dynamic-slice_fusion.3
  261.6 5.0 %fusion.55 = f32[32,4096]{1,0:T(8,128)S(1)} fusion(bf16[1024,4096]{1,0:T(8,128)(2,1)} %get-tuple-element.171, bf16[32,1024]{1,0:T(8,128)(2,1)S(1)} %get-tuple-element.157, bf16[32]{0:T(256)(128)(2,1)S(1)} %get-tuple-element.142), kind=kOutput, calls=%fused_computation.24.clone.1 | convolution fusion | flops 268468224 | bytes 8978496 | tf_op jit(solution)/shard_map/while/body/eval_jaxpr/dot_general | solution.py:46
  266.6 1.1 constant_dynamic-slice_fusion.3
  268.8 5.0 %fusion.55 = f32[32,4096]{1,0:T(8,128)S(1)} fusion(bf16[1024,4096]{1,0:T(8,128)(2,1)} %get-tuple-element.171, bf16[32,1024]{1,0:T(8,128)(2,1)S(1)} %get-tuple-element.157, bf16[32]{0:T(256)(128)(2,1)S(1)} %get-tuple-element.142), kind=kOutput, calls=%fused_computation.24.clone.1 | convolution fusion | flops 268468224 | bytes 8978496 | tf_op jit(solution)/shard_map/while/body/eval_jaxpr/dot_general | solution.py:46
  273.8 1.1 constant_dynamic-slice_fusion.3
  276.0 5.0 %fusion.55 = f32[32,4096]{1,0:T(8,128)S(1)} fusion(bf16[1024,4096]{1,0:T(8,128)(2,1)} %get-tuple-element.171, bf16[32,1024]{1,0:T(8,128)(2,1)S(1)} %get-tuple-element.157, bf16[32]{0:T(256)(128)(2,1)S(1)} %get-tuple-element.142), kind=kOutput, calls=%fused_computation.24.clone.1 | convolution fusion | flops 268468224 | bytes 8978496 | tf_op jit(solution)/shard_map/while/body/eval_jaxpr/dot_general | solution.py:46
  281.0 1.1 constant_dynamic-slice_fusion.3
  283.2 5.0 %fusion.55 = f32[32,4096]{1,0:T(8,128)S(1)} fusion(bf16[1024,4096]{1,0:T(8,128)(2,1)} %get-tuple-element.171, bf16[32,1024]{1,0:T(8,128)(2,1)S(1)} %get-tuple-element.157, bf16[32]{0:T(256)(128)(2,1)S(1)} %get-tuple-element.142), kind=kOutput, calls=%fused_computation.24.clone.1 | convolution fusion | flops 268468224 | bytes 8978496 | tf_op jit(solution)/shard_map/while/body/eval_jaxpr/dot_general | solution.py:46
  288.2 1.1 constant_dynamic-slice_fusion.3
  290.4 5.0 %fusion.55 = f32[32,4096]{1,0:T(8,128)S(1)} fusion(bf16[1024,4096]{1,0:T(8,128)(2,1)} %get-tuple-element.171, bf16[32,1024]{1,0:T(8,128)(2,1)S(1)} %get-tuple-element.157, bf16[32]{0:T(256)(128)(2,1)S(1)} %get-tuple-element.142), kind=kOutput, calls=%fused_computation.24.clone.1 | convolution fusion | flops 268468224 | bytes 8978496 | tf_op jit(solution)/shard_map/while/body/eval_jaxpr/dot_general | solution.py:46
  295.4 1.1 constant_dynamic-slice_fusion.3
  297.6 5.0 %fusion.55 = f32[32,4096]{1,0:T(8,128)S(1)} fusion(bf16[1024,4096]{1,0:T(8,128)(2,1)} %get-tuple-element.171, bf16[32,1024]{1,0:T(8,128)(2,1)S(1)} %get-tuple-element.157, bf16[32]{0:T(256)(128)(2,1)S(1)} %get-tuple-element.142), kind=kOutput, calls=%fused_computation.24.clone.1 | convolution fusion | flops 268468224 | bytes 8978496 | tf_op jit(solution)/shard_map/while/body/eval_jaxpr/dot_general | solution.py:46
  302.6 1.1 constant_dynamic-slice_fusion.3
  304.8 5.0 %fusion.55 = f32[32,4096]{1,0:T(8,128)S(1)} fusion(bf16[1024,4096]{1,0:T(8,128)(2,1)} %get-tuple-element.171, bf16[32,1024]{1,0:T(8,128)(2,1)S(1)} %get-tuple-element.157, bf16[32]{0:T(256)(128)(2,1)S(1)} %get-tuple-element.142), kind=kOutput, calls=%fused_computation.24.clone.1 | convolution fusion | flops 268468224 | bytes 8978496 | tf_op jit(solution)/shard_map/while/body/eval_jaxpr/dot_general | solution.py:46
  309.8 1.1 constant_dynamic-slice_fusion.3
  312.1 5.0 %fusion.55 = f32[32,4096]{1,0:T(8,128)S(1)} fusion(bf16[1024,4096]{1,0:T(8,128)(2,1)} %get-tuple-element.171, bf16[32,1024]{1,0:T(8,128)(2,1)S(1)} %get-tuple-element.157, bf16[32]{0:T(256)(128)(2,1)S(1)} %get-tuple-element.142), kind=kOutput, calls=%fused_computation.24.clone.1 | convolution fusion | flops 268468224 | bytes 8978496 | tf_op jit(solution)/shard_map/while/body/eval_jaxpr/dot_general | solution.py:46
  317.1 1.1 constant_dynamic-slice_fusion.3
  319.3 5.0 %fusion.55 = f32[32,4096]{1,0:T(8,128)S(1)} fusion(bf16[1024,4096]{1,0:T(8,128)(2,1)} %get-tuple-element.171, bf16[32,1024]{1,0:T(8,128)(2,1)S(1)} %get-tuple-element.157, bf16[32]{0:T(256)(128)(2,1)S(1)} %get-tuple-element.142), kind=kOutput, calls=%fused_computation.24.clone.1 | convolution fusion | flops 268468224 | bytes 8978496 | tf_op jit(solution)/shard_map/while/body/eval_jaxpr/dot_general | solution.py:46
  324.3 1.1 constant_dynamic-slice_fusion.3
  326.5 5.0 %fusion.55 = f32[32,4096]{1,0:T(8,128)S(1)} fusion(bf16[1024,4096]{1,0:T(8,128)(2,1)} %get-tuple-element.171, bf16[32,1024]{1,0:T(8,128)(2,1)S(1)} %get-tuple-element.157, bf16[32]{0:T(256)(128)(2,1)S(1)} %get-tuple-element.142), kind=kOutput, calls=%fused_computation.24.clone.1 | convolution fusion | flops 268468224 | bytes 8978496 | tf_op jit(solution)/shard_map/while/body/eval_jaxpr/dot_general | solution.py:46
  331.5 1.1 constant_dynamic-slice_fusion.3
  333.7 5.0 %fusion.55 = f32[32,4096]{1,0:T(8,128)S(1)} fusion(bf16[1024,4096]{1,0:T(8,128)(2,1)} %get-tuple-element.171, bf16[32,1024]{1,0:T(8,128)(2,1)S(1)} %get-tuple-element.157, bf16[32]{0:T(256)(128)(2,1)S(1)} %get-tuple-element.142), kind=kOutput, calls=%fused_computation.24.clone.1 | convolution fusion | flops 268468224 | bytes 8978496 | tf_op jit(solution)/shard_map/while/body/eval_jaxpr/dot_general | solution.py:46
  338.7 1.1 constant_dynamic-slice_fusion.3
  341.0 5.0 %fusion.55 = f32[32,4096]{1,0:T(8,128)S(1)} fusion(bf16[1024,4096]{1,0:T(8,128)(2,1)} %get-tuple-element.171, bf16[32,1024]{1,0:T(8,128)(2,1)S(1)} %get-tuple-element.157, bf16[32]{0:T(256)(128)(2,1)S(1)} %get-tuple-element.142), kind=kOutput, calls=%fused_computation.24.clone.1 | convolution fusion | flops 268468224 | bytes 8978496 | tf_op jit(solution)/shard_map/while/body/eval_jaxpr/dot_general | solution.py:46
  345.9 1.1 constant_dynamic-slice_fusion.3
  348.2 5.0 %fusion.55 = f32[32,4096]{1,0:T(8,128)S(1)} fusion(bf16[1024,4096]{1,0:T(8,128)(2,1)} %get-tuple-element.171, bf16[32,1024]{1,0:T(8,128)(2,1)S(1)} %get-tuple-element.157, bf16[32]{0:T(256)(128)(2,1)S(1)} %get-tuple-element.142), kind=kOutput, calls=%fused_computation.24.clone.1 | convolution fusion | flops 268468224 | bytes 8978496 | tf_op jit(solution)/shard_map/while/body/eval_jaxpr/dot_general | solution.py:46
  353.1 1.1 constant_dynamic-slice_fusion.3
  355.4 5.0 %fusion.55 = f32[32,4096]{1,0:T(8,128)S(1)} fusion(bf16[1024,4096]{1,0:T(8,128)(2,1)} %get-tuple-element.171, bf16[32,1024]{1,0:T(8,128)(2,1)S(1)} %get-tuple-element.157, bf16[32]{0:T(256)(128)(2,1)S(1)} %get-tuple-element.142), kind=kOutput, calls=%fused_computation.24.clone.1 | convolution fusion | flops 268468224 | bytes 8978496 | tf_op jit(solution)/shard_map/while/body/eval_jaxpr/dot_general | solution.py:46
  360.4 1.1 constant_dynamic-slice_fusion.3
  362.6 5.0 %fusion.55 = f32[32,4096]{1,0:T(8,128)S(1)} fusion(bf16[1024,4096]{1,0:T(8,128)(2,1)} %get-tuple-element.171, bf16[32,1024]{1,0:T(8,128)(2,1)S(1)} %get-tuple-element.157, bf16[32]{0:T(256)(128)(2,1)S(1)} %get-tuple-element.142), kind=kOutput, calls=%fused_computation.24.clone.1 | convolution fusion | flops 268468224 | bytes 8978496 | tf_op jit(solution)/shard_map/while/body/eval_jaxpr/dot_general | solution.py:46
  367.6 1.1 constant_dynamic-slice_fusion.3
  369.8 5.0 %fusion.55 = f32[32,4096]{1,0:T(8,128)S(1)} fusion(bf16[1024,4096]{1,0:T(8,128)(2,1)} %get-tuple-element.171, bf16[32,1024]{1,0:T(8,128)(2,1)S(1)} %get-tuple-element.157, bf16[32]{0:T(256)(128)(2,1)S(1)} %get-tuple-element.142), kind=kOutput, calls=%fused_computation.24.clone.1 | convolution fusion | flops 268468224 | bytes 8978496 | tf_op jit(solution)/shard_map/while/body/eval_jaxpr/dot_general | solution.py:46
  374.8 1.1 constant_dynamic-slice_fusion.3
  377.0 5.0 %fusion.55 = f32[32,4096]{1,0:T(8,128)S(1)} fusion(bf16[1024,4096]{1,0:T(8,128)(2,1)} %get-tuple-element.171, bf16[32,1024]{1,0:T(8,128)(2,1)S(1)} %get-tuple-element.157, bf16[32]{0:T(256)(128)(2,1)S(1)} %get-tuple-element.142), kind=kOutput, calls=%fused_computation.24.clone.1 | convolution fusion | flops 268468224 | bytes 8978496 | tf_op jit(solution)/shard_map/while/body/eval_jaxpr/dot_general | solution.py:46
  382.0 1.1 constant_dynamic-slice_fusion.3
  384.2 5.0 %fusion.55 = f32[32,4096]{1,0:T(8,128)S(1)} fusion(bf16[1024,4096]{1,0:T(8,128)(2,1)} %get-tuple-element.171, bf16[32,1024]{1,0:T(8,128)(2,1)S(1)} %get-tuple-element.157, bf16[32]{0:T(256)(128)(2,1)S(1)} %get-tuple-element.142), kind=kOutput, calls=%fused_computation.24.clone.1 | convolution fusion | flops 268468224 | bytes 8978496 | tf_op jit(solution)/shard_map/while/body/eval_jaxpr/dot_general | solution.py:46
  389.2 1.1 constant_dynamic-slice_fusion.3
  391.5 5.0 %fusion.55 = f32[32,4096]{1,0:T(8,128)S(1)} fusion(bf16[1024,4096]{1,0:T(8,128)(2,1)} %get-tuple-element.171, bf16[32,1024]{1,0:T(8,128)(2,1)S(1)} %get-tuple-element.157, bf16[32]{0:T(256)(128)(2,1)S(1)} %get-tuple-element.142), kind=kOutput, calls=%fused_computation.24.clone.1 | convolution fusion | flops 268468224 | bytes 8978496 | tf_op jit(solution)/shard_map/while/body/eval_jaxpr/dot_general | solution.py:46
  396.4 1.1 constant_dynamic-slice_fusion.3
  398.7 5.0 %fusion.55 = f32[32,4096]{1,0:T(8,128)S(1)} fusion(bf16[1024,4096]{1,0:T(8,128)(2,1)} %get-tuple-element.171, bf16[32,1024]{1,0:T(8,128)(2,1)S(1)} %get-tuple-element.157, bf16[32]{0:T(256)(128)(2,1)S(1)} %get-tuple-element.142), kind=kOutput, calls=%fused_computation.24.clone.1 | convolution fusion | flops 268468224 | bytes 8978496 | tf_op jit(solution)/shard_map/while/body/eval_jaxpr/dot_general | solution.py:46
  403.6 1.1 constant_dynamic-slice_fusion.3
  405.9 5.0 %fusion.55 = f32[32,4096]{1,0:T(8,128)S(1)} fusion(bf16[1024,4096]{1,0:T(8,128)(2,1)} %get-tuple-element.171, bf16[32,1024]{1,0:T(8,128)(2,1)S(1)} %get-tuple-element.157, bf16[32]{0:T(256)(128)(2,1)S(1)} %get-tuple-element.142), kind=kOutput, calls=%fused_computation.24.clone.1 | convolution fusion | flops 268468224 | bytes 8978496 | tf_op jit(solution)/shard_map/while/body/eval_jaxpr/dot_general | solution.py:46
  410.8 1.1 constant_dynamic-slice_fusion.3
  413.1 2.0 convolution_convert_fusion
  415.1 2.2 reshape.110
  417.4 3.8 copy.48
  421.1 28.5 %all_to_all.35 = bf16[32,2,16,1024]{3,1,2,0:T(2,128)(2,1)S(1)} all-to-all(bf16[32,2,16,1024]{3,1,2,0:T(2,128)(2,1)S(1)} %copy.48), channel_id=1, replica_groups=mesh['batch'=32,'head'=4] {'head'}, dimensions={0} | all-to-all | bytes 4194304 | tf_op jit(solution)/shard_map/all_to_all | solution.py:100
  450.3 8.3 %maximum_convert_fusion = bf16[8,128,1024]{2,1,0:T(8,128)(2,1)S(1)} fusion(bf16[8,128,1024]{2,1,0:T(8,128)(2,1)S(1)} %bitcast.89, bf16[8,1024,1024]{2,1,0:T(8,128)(2,1)} %param.25), kind=kOutput, calls=%fused_computation.31 | convolution fusion | flops 2149580800 | bytes 20971520 | tf_op jit(solution)/shard_map/prh,phk->prk/dot_general | solution.py:103
  460.6 6.6 %all_to_all.36 = bf16[4,2,2304]{2,1,0:T(2,128)(2,1)S(1)} all-to-all(bf16[4,2,2304]{2,1,0:T(2,128)(2,1)S(1)} %reshape.118), channel_id=1, replica_groups=mesh['batch'=32,'head'=4] {'head'}, dimensions={0} | all-to-all | bytes 73728 | tf_op jit(solution)/shard_map/all_to_all | solution.py:114
  (121 shorter events, 35.1 us)
Async XLA Ops:
  7.2 451.4 %copy-start = (bf16[8,512,18]{1,0,2:T(8,128)(2,1)S(1)}, bf16[8,512,18]{1,0,2:T(8,128)(2,1)}, u32[]{:S(2)}) copy-start(bf16[8,512,18]{1,0,2:T(8,128)(2,1)} %param.27) | copy-start | bytes 442372
  7.2 181.4 %all-gather.2.cloned.1.call-start = ((), (), s32[]{:S(2)}) async-start(), calls=%async_computation.3 | async-start | bytes 4325376 | tf_op jit(solution)/shard_map/all_gather | solution.py:80
  24.0 10.8 %copy-start.1 = (bf16[32,24,512]{2,1,0:T(8,128)(2,1)S(1)}, bf16[32,24,512]{2,1,0:T(8,128)(2,1)}, u32[]{:S(2)}) copy-start(bf16[32,24,512]{2,1,0:T(8,128)(2,1)} %param.15) | copy-start | bytes 2359300
  24.0 11.0 %copy-start.9 = (s32[32]{0:T(128)S(1)}, s32[32]{0:T(128)}, u32[]{:S(2)}) copy-start(s32[32]{0:T(128)} %param.18) | copy-start | bytes 388
  24.0 11.0 %copy-start.7 = (s32[32,1]{0,1:T(1,128)S(1)}, s32[32,1]{0,1:T(1,128)}, u32[]{:S(2)}) copy-start(s32[32,1]{0,1:T(1,128)} %param.20) | copy-start | bytes 388
  24.0 11.2 %copy-start.5 = (s32[32,24]{0,1:T(8,128)S(1)}, s32[32,24]{0,1:T(8,128)}, u32[]{:S(2)}) copy-start(s32[32,24]{0,1:T(8,128)} %param.19) | copy-start | bytes 9220
  24.0 11.2 %copy-start.3 = (bf16[32,1024]{1,0:T(8,128)(2,1)S(1)}, bf16[32,1024]{1,0:T(8,128)(2,1)}, u32[]{:S(2)}) copy-start(bf16[32,1024]{1,0:T(8,128)(2,1)} %param.17) | copy-start | bytes 196612
  24.1 11.2 %copy-start.4 = (bf16[32,1024]{1,0:T(8,128)(2,1)S(1)}, bf16[32,1024]{1,0:T(8,128)(2,1)}, u32[]{:S(2)}) copy-start(bf16[32,1024]{1,0:T(8,128)(2,1)} %param.16) | copy-start | bytes 196612
  24.1 203.7 %all-to-all-start = ((bf16[32,32,4,1024]{3,2,1,0:T(4,128)(2,1)}), bf16[32,32,4,1024]{3,2,1,0:T(4,128)(2,1)}, u32[]{:S(2)}, u32[]{:S(2)}) async-start(bf16[32,32,4,1024]{3,2,1,0:T(4,128)(2,1)} %stack.2), calls=%async_computation | async-start | bytes 16777216 | tf_op jit(solution)/shard_map/all_to_all | solution.py:15
  227.8 12.1 %copy-start.2 = (f32[4,1024]{1,0:T(4,128)S(1)}, f32[4,1024]{1,0:T(4,128)}, u32[]{:S(2)}) copy-start(f32[4,1024]{1,0:T(4,128)} %param.24) | copy-start | bytes 49156
  450.3 8.7 %copy-start.8 = (bf16[8,512]{1,0:T(8,128)(2,1)S(1)}, bf16[8,512]{1,0:T(8,128)(2,1)}, u32[]{:S(2)}) copy-start(bf16[8,512]{1,0:T(8,128)(2,1)} %param.26) | copy-start | bytes 24580
  458.6 9.6 %copy-start.6 = (s32[32,16]{0,1:T(8,128)S(1)}, s32[32,16]{0,1:T(8,128)}, u32[]{:S(2)}) copy-start(s32[32,16]{0,1:T(8,128)} %param.21) | copy-start | bytes 6148
Sparse Core Ops, SparseCore 0:
  16.9 171.6 all-gather.1
